TPU v7x, 128 devices: a whole 4x4x4 slice. The times are simulated.
128 devices in a mesh: dp: 8 (over y, x_lo), tensor: 16 (over x_hi, z, core).
Axes of the slice: x: 4 (x_hi: 2, x_lo: 2; x = x_hi * 2 + x_lo), y: 4, z: 4, core: 2. Of those that a mesh axis runs over, the one named last changes fastest.
Arguments:
- grad_out: bfloat16 [8192, 8192], P(('dp', 'tensor')), may hold values from -24 to 24
- out_weight: bfloat16 [8192, 8192], P('dp', 'tensor'), may hold values from -0.0625 to 0.0625
- query: bfloat16 [8192, 8192], P('dp', 'tensor'), may hold values from -6 to 6, as said below
- keys: bfloat16 [8192, 512], P('dp'), may hold values from -6 to 6
- values: bfloat16 [8192, 512], P('dp'), may hold values from -6 to 6
- attended: bfloat16 [8192, 8192], P('dp', 'tensor'), may hold values from -6 to 6, as said below
- stats: float32 [64, 8192], P('tensor', 'dp'), as said below
Outputs:
- query_grad: bfloat16 [8192, 8192], P('dp', 'tensor')
- key_grad: bfloat16 [8192, 512], P('dp', 'tensor')
- value_grad: bfloat16 [8192, 512], P('dp', 'tensor')
- weight_grad: bfloat16 [8192, 8192], P('dp', 'tensor')
Inputs may be any that keep to these rules, and one draw needn't show every extreme that they name: query, keys and values are independent draws. attended is the causal attention output of the given query, keys and values within each sequence of 1024 rows: query head h uses key head h // 16, scores scaled by 128 ** -0.5, softmax over keys at or before the query. stats[h, t] is the logarithm of the sum of exp(score) over the keys that row t of head h attends to, for the same scores.
All inputs are finite; a program needn't handle non-finite values.
Results may differ from a plain program's by a relative error of at most 0.013.
Values may be sent and summed in bfloat16 or wider, within the bound.
A program may use at most 192 MiB of HBM per device.

v0:
```python
import jax
import jax.numpy as jnp
from jax import lax
from jax.sharding import Mesh
from jax.sharding import PartitionSpec as P

HD = 128
HEAD_DEV = 4
GROUP = 16
DP = ("dp_0", "dp_1")
DP_TENSOR = ("dp_0", "dp_1", "tensor")


def gathered_by_axis(x, axes, dim):
    if not axes:
        return x
    nearer = lax.all_gather(x, axes[-1], axis=dim, tiled=True)
    return gathered_by_axis(nearer, axes[:-1], dim)


def sum_by_axis(terms, axes):
    subtotal = terms.astype(jnp.bfloat16)
    for axis in axes:
        subtotal = lax.psum_scatter(subtotal, axis, scatter_dimension=0, tiled=True)
    return subtotal.astype(jnp.float32)


def partner(value, axis, apart):
    mask = 2**apart
    pairs = [(source, source ^ mask) for source in range(lax.axis_size(axis))]
    return lax.ppermute(value, axis, pairs)


def attention_grads(query, key_one, value_one, attended, grad_att, stats):
    length = query.shape[0]
    score_scale = HD ** (-0.5)
    query_heads = query.reshape(length, HEAD_DEV, HD)
    grad_heads = grad_att.reshape(length, HEAD_DEV, HD)
    attended_heads = attended.reshape(length, HEAD_DEV, HD)
    positions = jnp.arange(length, dtype=jnp.int32)
    causal = positions[:, None] >= positions[None, :]
    scores = (
        jnp.einsum("qgd,kd->gqk", query_heads, key_one, preferred_element_type=jnp.float32)
        * score_scale
    )
    attention = jnp.where(causal[None], jnp.exp(scores - stats[:, :, None]), 0.0)
    attention_low = attention.astype(jnp.bfloat16)
    grad_attention = jnp.einsum(
        "qgd,kd->gqk", grad_heads, value_one, preferred_element_type=jnp.float32
    )
    row_offset = jnp.sum(
        grad_heads.astype(jnp.float32) * attended_heads.astype(jnp.float32), axis=2
    )
    grad_scores = (attention * (grad_attention - row_offset.T[:, :, None])).astype(jnp.bfloat16)
    query_grad = (
        jnp.einsum("gqk,kd->qgd", grad_scores, key_one, preferred_element_type=jnp.float32)
        * score_scale
    )
    query_grad = query_grad.astype(jnp.bfloat16).reshape(length, HEAD_DEV * HD)
    key_part = (
        jnp.einsum("gqk,qgd->kd", grad_scores, query_heads, preferred_element_type=jnp.float32)
        * score_scale
    )
    value_part = jnp.einsum(
        "gqk,qgd->kd", attention_low, grad_heads, preferred_element_type=jnp.float32
    )
    return (query_grad, key_part, value_part)


def per_device(grad_out, out_weight, query, keys, values, attended, stats):
    grad_rows = lax.all_gather(grad_out, "tensor", axis=0, tiled=True)
    grad_block = grad_rows
    grad_att = jnp.dot(
        grad_block, gathered_by_axis(out_weight, DP, 0), preferred_element_type=jnp.float32
    ).astype(jnp.bfloat16)
    grad_block = grad_rows
    weight_grad = sum_by_axis(
        lax.dot_general(
            grad_block, attended, (((0,), (0,)), ((), ())), preferred_element_type=jnp.float32
        ),
        DP,
    ).astype(jnp.bfloat16)
    tensor_index = lax.axis_index("tensor")
    key_head = tensor_index * HEAD_DEV // GROUP
    key_one = lax.dynamic_slice_in_dim(keys, key_head * HD, HD, 1)
    value_one = lax.dynamic_slice_in_dim(values, key_head * HD, HD, 1)
    query_grad, key_part, value_part = attention_grads(
        query, key_one, value_one, attended, grad_att, stats
    )
    group_span = GROUP // HEAD_DEV
    group_place = tensor_index % group_span
    bit_count = group_span.bit_length() - 1
    running_kv = jnp.stack([key_part, value_part])
    for bit_number in reversed(range(bit_count)):
        half_cols = running_kv.shape[2] // 2
        lower_cols = running_kv[:, :, :half_cols]
        upper_cols = running_kv[:, :, half_cols:]
        upper_half = group_place // (1 << bit_number) % 2 == 1
        kept_cols = jnp.where(upper_half, upper_cols, lower_cols)
        sent_cols = jnp.where(upper_half, lower_cols, upper_cols)
        running_kv = kept_cols + partner(
            sent_cols.astype(jnp.bfloat16), "tensor", bit_number
        ).astype(sent_cols.dtype)
    key_grad = running_kv[0].astype(jnp.bfloat16)
    value_grad = running_kv[1].astype(jnp.bfloat16)
    return (query_grad, key_grad, value_grad, weight_grad)


def solution(mesh):
    torus = Mesh(mesh.devices.reshape(4, 2, mesh.shape["tensor"]), ("dp_0", "dp_1", "tensor"))
    in_specs = (
        P(DP_TENSOR, None),
        P(DP, "tensor"),
        P(DP, "tensor"),
        P(DP, None),
        P(DP, None),
        P(DP, "tensor"),
        P("tensor", DP),
    )
    out_specs = (P(DP, "tensor"), P(DP, "tensor"), P(DP, "tensor"), P(DP, "tensor"))
    return jax.shard_map(
        per_device, mesh=torus, in_specs=in_specs, out_specs=out_specs, check_vma=False
    )
```

profile of v0, /device:TPU:1, one launch (start us, length us, event | category | flops | bytes accessed | tf_op | source)
XLA Modules:
  0.0 373.3 jit_solution(7424440204434012823)
XLA Ops:
  7.2 0.0 copy-start
  7.2 0.0 all-gather.6.cloned.1.call-start
  7.2 0.7 all-gather.6.cloned.1.call-update
  7.9 0.0 all-gather.4.cloned.1.call-start
  8.0 0.7 all-gather.4.cloned.1.call-update
  8.7 0.0 all-gather.8.cloned.1.call-start
  8.7 39.6 %all-gather.6.cloned.1.call-done = bf16[2048,512]{1,0:T(8,128)(2,1)} async-done(((bf16[1024,512]{1,0:T(8,128)(2,1)}), bf16[2048,512]{1,0:T(8,128)(2,1)}) %all-gather.6.cloned.1.call-update) | async-done | bytes 2097168 | tf_op jit(solution)/shard_map/all_gather | solution.py:17
  48.3 0.0 all-gather.8.cloned.1.call-update
  48.3 0.0 copy-start.1
  48.3 0.0 copy-start.2
  48.4 0.0 reduce-scatter.3.cloned.1.call-start
  48.4 112.8 %all-gather.4.cloned.1.call-done = bf16[1024,8192]{1,0:T(8,128)(2,1)} async-done(((bf16[64,8192]{1,0:T(8,128)(2,1)}), bf16[1024,8192]{1,0:T(8,128)(2,1)}) %all-gather.4.cloned.1.call-update) | async-done | bytes 16777232 | tf_op jit(solution)/shard_map/all_gather | solution.py:71
  161.2 14.8 %convolution_convert_fusion = bf16[8192,512]{1,0:T(8,128)(2,1)} fusion(bf16[1024,8192]{1,0:T(8,128)(2,1)} %all-gather.4.cloned.1.call-done, bf16[1024,512]{1,0:T(8,128)(2,1)} %param.12), kind=kOutput, calls=%fused_computation.7 | convolution fusion | flops 8594128896 | bytes 26214400 | tf_op jit(solution)/shard_map/dot_general | solution.py:78
  176.0 0.0 reduce-scatter.3.cloned.1.call-update
  176.0 0.2 reduce-scatter.5.cloned.1.call-start
  176.3 0.0 copy-done.1
  176.3 1.6 copy.26
  177.9 0.0 copy-done.2
  177.9 0.5 copy.27
  178.4 0.3 iota_compare_fusion
  178.7 0.0 copy-start.3
  178.8 0.0 copy-done
  178.8 8.1 %fusion.15 = f32[1024,1024,4]{1,0,2:T(8,128)} fusion(bf16[1024,4,128]{0,2,1:T(8,128)(2,1)S(1)} %bitcast.65, bf16[1024,512]{1,0:T(8,128)(2,1)S(1)} %copy-done, s32[]{:T(128)S(6)} %select_n.56), kind=kOutput, calls=%fused_computation.25 | convolution fusion | flops 1073741824 | bytes 18087940 | tf_op jit(solution)/shard_map/qgd,kd->gqk/dot_general | solution.py:43
  186.9 56.2 %all-gather.8.cloned.1.call-done = bf16[8192,512]{1,0:T(8,128)(2,1)} async-done(((bf16[2048,512]{1,0:T(8,128)(2,1)}), bf16[8192,512]{1,0:T(8,128)(2,1)}) %all-gather.8.cloned.1.call-update) | async-done | bytes 8388624 | tf_op jit(solution)/shard_map/all_gather | solution.py:17
  243.0 15.6 %multiply_reduce_fusion = (f32[1024,4]{0,1:T(4,128)S(1)}, bf16[1024,512]{0,1:T(8,128)(2,1)}) fusion(f32[1024,512]{0,1:T(8,128)} %copy.26, bf16[1024,8192]{1,0:T(8,128)(2,1)} %all-gather.4.cloned.1.call-done, bf16[8192,512]{1,0:T(8,128)(2,1)} %all-gather.8.cloned.1.call-done), kind=kOutput, calls=%fused_computation.12 | convolution fusion | flops 8592027648 | bytes 28327936 | tf_op jit(solution)/shard_map/dot_general | solution.py:73
  258.6 68.3 %reduce-scatter.3.cloned.1.call-done = bf16[2048,512]{1,0:T(8,128)(2,1)} async-done(((bf16[8192,512]{1,0:T(8,128)(2,1)}), bf16[2048,512]{1,0:T(8,128)(2,1)}) %reduce-scatter.3.cloned.1.call-update) | async-done | bytes 2097168 | tf_op jit(solution)/shard_map/reduce_scatter | solution.py:24
  326.9 0.0 reduce-scatter.5.cloned.1.call-update
  327.0 0.0 slice-start
  327.0 0.0 slice-start.1
  327.0 0.0 slice-start.2
  327.0 0.0 copy-start.5
  327.0 11.5 %fusion.1 = bf16[4,1024,1024]{1,2,0:T(8,128)(2,1)} fusion(f32[1024,1024,4]{1,0,2:T(8,128)} %fusion.15, bf16[1024,4,128]{0,2,1:T(8,128)(2,1)} %bitcast.67, f32[4,1024]{1,0:T(4,128)S(1)} %bitcast.69, f32[4,1024]{1,0:T(4,128)S(1)} %copy-done.4, pred[1024,1024]{0,1:T(8,128)(4,1)S(1)} %iota_compare_fusion, bf16[1024,512]{1,0:T(8,128)(2,1)} %param.11, ...), kind=kOutput, calls=%fused_computation.2 | convolution fusion | flops 1098907648 | bytes 27557892 | tf_op jit(solution)/shard_map/qgd,kd->gqk/dot_general | solution.py:48
  338.5 7.2 %fusion.9 = f32[1,1024,128]{1,2,0:T(8,128)S(1)} fusion(bf16[4,1024,1024]{1,2,0:T(8,128)(2,1)} %fusion.1, bf16[1024,4,128]{0,2,1:T(8,128)(2,1)S(1)} %bitcast.66), kind=kOutput, calls=%fused_computation.16 | convolution fusion | flops 1073872896 | bytes 9961472 | tf_op jit(solution)/shard_map/gqk,qgd->kd/dot_general | solution.py:61
  345.7 0.0 slice-done
  345.7 0.0 slice-done.1
  345.7 0.0 slice-done.2
  345.7 0.0 copy-done.5
  345.7 0.0 slice-done.3
  345.7 5.2 %fusion.10 = f32[1,1024,128]{1,2,0:T(8,128)S(1)} fusion(bf16[1024,4,128]{0,2,1:T(8,128)(2,1)S(1)} %bitcast.68, f32[1024,1024,4]{1,0,2:T(8,128)S(1)} %bitcast.63, f32[4,1024]{1,0:T(4,128)S(1)} %copy-done.4, pred[1024,1024]{0,1:T(8,128)(4,1)} %copy-done.3), kind=kOutput, calls=%fused_computation.17 | convolution fusion | flops 1090519040 | bytes 19415040 | tf_op jit(solution)/shard_map/gqk,qgd->kd/dot_general | solution.py:64
  351.0 0.1 select_convert_fusion
  351.0 1.5 collective-permute-start
  352.5 6.0 %collective-permute-done = bf16[2,1024,64]{1,2,0:T(8,128)(2,1)S(1)} collective-permute-done((bf16[2,1024,64]{1,2,0:T(8,128)(2,1)S(1)}, bf16[2,1024,64]{1,2,0:T(8,128)(2,1)S(1)}, u32[]{:S(2)}, u32[]{:S(2)}) %collective-permute-start) | collective-permute-done | bytes 262176 | tf_op jit(solution)/shard_map/ppermute | solution.py:31
  358.4 0.1 convert_add_fusion
  358.6 1.5 collective-permute-start.1
  360.0 4.7 %multiply_convert_fusion = bf16[128,4,1024]{2,0,1:T(8,128)(2,1)S(1)} fusion(bf16[4,1024,1024]{1,2,0:T(8,128)(2,1)} %fusion.1, bf16[1024,512]{1,0:T(8,128)(2,1)S(1)} %copy-done, s32[]{:T(128)S(6)} %select_n.56), kind=kOutput, calls=%fused_computation.11 | convolution fusion | flops 1074790400 | bytes 9699332 | tf_op jit(solution)/shard_map/gqk,kd->qgd/dot_general | solution.py:56
  364.7 1.3 copy.19
  366.1 0.0 collective-permute-done.1
  366.1 0.7 slice_bitcast_fusion
  (8 shorter events, 0.1 us)
Async XLA Ops:
  7.2 171.6 %copy-start = (bf16[1024,512]{1,0:T(8,128)(2,1)S(1)}, bf16[1024,512]{1,0:T(8,128)(2,1)}, u32[]{:S(2)}) copy-start(bf16[1024,512]{1,0:T(8,128)(2,1)} %param.10) | copy-start | bytes 3145732
  7.2 41.1 %all-gather.6.cloned.1.call-start = ((), (), s32[]{:S(2)}) async-start(), calls=%async_computation.3 | async-start | bytes 3145728 | tf_op jit(solution)/shard_map/all_gather | solution.py:17
  7.9 153.3 %all-gather.4.cloned.1.call-start = ((), (), s32[]{:S(2)}) async-start(), calls=%async_computation.2 | async-start | bytes 17825792 | tf_op jit(solution)/shard_map/all_gather | solution.py:71
  8.7 234.3 %all-gather.8.cloned.1.call-start = ((), (), s32[]{:S(2)}) async-start(), calls=%async_computation.4 | async-start | bytes 10485760 | tf_op jit(solution)/shard_map/all_gather | solution.py:17
  48.3 127.9 %copy-start.1 = (bf16[1024,512]{1,0:T(8,128)(2,1)S(1)}, bf16[1024,512]{1,0:T(8,128)(2,1)}, u32[]{:S(2)}) copy-start(bf16[1024,512]{1,0:T(8,128)(2,1)} %param.12) | copy-start | bytes 3145732
  48.3 129.5 %copy-start.2 = (bf16[1024,512]{1,0:T(8,128)(2,1)S(1)}, bf16[1024,512]{1,0:T(8,128)(2,1)}, u32[]{:S(2)}) copy-start(bf16[1024,512]{1,0:T(8,128)(2,1)} %param.9) | copy-start | bytes 3145732
  48.4 278.6 %reduce-scatter.3.cloned.1.call-start = ((), (), s32[]{:S(2)}) async-start(), calls=%async_computation.5 | async-start | bytes 10485760 | tf_op jit(solution)/shard_map/reduce_scatter | solution.py:24
  176.0 190.8 %reduce-scatter.5.cloned.1.call-start = ((), (), s32[]{:S(2)}) async-start(), calls=%async_computation.6 | async-start | bytes 3145728 | tf_op jit(solution)/shard_map/reduce_scatter | solution.py:24
  178.7 148.2 %copy-start.3 = (pred[1024,1024]{0,1:T(8,128)(4,1)}, pred[1024,1024]{0,1:T(8,128)(4,1)S(1)}, u32[]{:S(2)}) copy-start(pred[1024,1024]{0,1:T(8,128)(4,1)S(1)} %iota_compare_fusion) | copy-start | bytes 3145732
  186.9 140.1 %copy-start.4 = (f32[4,1024]{1,0:T(4,128)S(1)}, f32[4,1024]{1,0:T(4,128)}, u32[]{:S(2)}) copy-start(f32[4,1024]{1,0:T(4,128)} %param.13) | copy-start | bytes 49156
  327.0 18.7 %slice-start = ((s8[16777216]{0:T(1024)(128)(4,1)}), s8[4194304]{0:T(1024)(128)(4,1)S(1)}, s32[]{:S(2)}) async-start(s8[16777216]{0:T(1024)(128)(4,1)} %bitcast.62), calls=%async_computation.7 | async-start | bytes 8388608
  327.0 18.7 %slice-start.1 = ((s8[16777216]{0:T(1024)(128)(4,1)}), s8[4194304]{0:T(1024)(128)(4,1)S(1)}, s32[]{:S(2)}) async-start(s8[16777216]{0:T(1024)(128)(4,1)} %bitcast.62), calls=%async_computation.8 | async-start | bytes 8388608
  327.0 18.7 %slice-start.2 = ((s8[16777216]{0:T(1024)(128)(4,1)}), s8[4194304]{0:T(1024)(128)(4,1)S(1)}, s32[]{:S(2)}) async-start(s8[16777216]{0:T(1024)(128)(4,1)} %bitcast.62), calls=%async_computation.9 | async-start | bytes 8388608
  327.0 18.7 %copy-start.5 = (bf16[1024,512]{0,1:T(8,128)(2,1)S(1)}, bf16[1024,512]{0,1:T(8,128)(2,1)}, u32[]{:S(2)}) copy-start(bf16[1024,512]{0,1:T(8,128)(2,1)} %get-tuple-element.11) | copy-start | bytes 3145732
  338.5 7.2 %slice-start.3 = ((s8[16777216]{0:T(1024)(128)(4,1)}), s8[4194304]{0:T(1024)(128)(4,1)S(1)}, s32[]{:S(2)}) async-start(s8[16777216]{0:T(1024)(128)(4,1)} %bitcast.62), calls=%async_computation.10 | async-start | bytes 8388608
  351.0 7.4 %collective-permute-start = (bf16[2,1024,64]{1,2,0:T(8,128)(2,1)S(1)}, bf16[2,1024,64]{1,2,0:T(8,128)(2,1)S(1)}, u32[]{:S(2)}, u32[]{:S(2)}) collective-permute-start(bf16[2,1024,64]{1,2,0:T(8,128)(2,1)S(1)} %select_convert_fusion), channel_id=1, source_target_pairs={{0,2},{1,3},{2,0},{3,1},{4,6},{5,7},{6,4},{7,5},{8,10},{9,11},{10,... | collective-permute-start | bytes 786440 | tf_op jit(solution)/shard_map/ppermute | solution.py:31
  358.6 7.5 %collective-permute-start.1 = (bf16[2,1024,32]{1,2,0:T(8,128)(2,1)S(1)}, bf16[2,1024,32]{1,2,0:T(8,128)(2,1)S(1)}, u32[]{:S(2)}, u32[]{:S(2)}) collective-permute-start(bf16[2,1024,32]{1,2,0:T(8,128)(2,1)S(1)} %select_convert_fusion.1), channel_id=1, source_target_pairs={{0,1},{1,0},{2,3},{3,2},{4,5},{5,4},{6,7},{7,6},{8,9},{9,8},{10,11... | collective-permute-start | bytes 393224 | tf_op jit(solution)/shard_map/ppermute | solution.py:31
Sparse Core Ops, SparseCore 0:
  9.6 38.6 all-gather.5
  50.8 110.3 all-gather.3
  162.9 80.0 all-gather.7
  245.3 81.5 reduce-scatter.2
  329.7 34.0 reduce-scatter.4
where the time goes:
time: 373 us
  waiting for transfers between devices  284 us (76%)
  matrix products  67 us (18%)
  between operations  14 us (4%)
  local copies, waits for them, and re-layouts  4.17 us (1%)
    all_gather x1, waiting for transfers between devices, per_device(): grad_rows = lax.all_gather(grad_out, 'tensor', axis=0, tiled=True)  113 us
    all_gather x2, waiting for transfers between devices, gathered_by_axis(): nearer = lax.all_gather(x, axes[-1], axis=dim, tiled=True)  95.7 us
    reduce_scatter x2, waiting for transfers between devices, sum_by_axis(): subtotal = lax.psum_scatter(subtotal, axis, scatter_dimension=0, tiled=True)  68.3 us
    dot_general x1, matrix products, per_device(): jnp.dot(grad_block, gathered_by_axis(out_weight, DP, 0), preferred_elemen...  15.6 us
    dot_general x1, matrix products, per_device(): lax.dot_general(grad_block, attended, (((0,), (0,)), ((), ())), preferred...  14.8 us
    dot_general x1, matrix products, attention_grads(): jnp.einsum('qgd,kd->gqk', grad_heads, value_one, preferred_element_type=j...  11.5 us
    dot_general x1, matrix products, attention_grads(): jnp.einsum('qgd,kd->gqk', query_heads, key_one, preferred_element_type=jn...  8.09 us
  transfers between devices with their start and end apart: 7, of which 5 were waited for; matrix products, arithmetic and copies ran while one was open for 19% of the time, Pallas kernels for 0%

commit v1 on v0

--- a/solution.py
+++ b/solution.py
@@ -68,7 +68,9 @@
 
 
 def per_device(grad_out, out_weight, query, keys, values, attended, stats):
-    grad_rows = lax.all_gather(grad_out, "tensor", axis=0, tiled=True)
+    grad_rows = jnp.concatenate(
+        lax.all_to_all(jnp.stack([grad_out] * lax.axis_size("tensor")), "tensor", 0, 0), axis=0
+    )
     grad_block = grad_rows
     grad_att = jnp.dot(
         grad_block, gathered_by_axis(out_weight, DP, 0), preferred_element_type=jnp.float32

time: 373 us -> 451 us (1.21)
  waiting for transfers between devices: 284 us -> 342 us
  starting transfers between devices: 3.3 us -> 12.7 us
  local copies, waits for them, and re-layouts: 4.17 us -> 11.1 us
    all_to_all x0 -> x1, waiting for transfers between devices: none -> 201 us  [per_device(): lax.all_to_all(jnp.stack([grad_out] * lax.axis_size('tensor')), 'tensor',...]
    all_gather x1 -> x0, waiting for transfers between devices: 113 us -> none  [per_device(): grad_rows = lax.all_gather(grad_out, 'tensor', axis=0, tiled=True)]
    all_gather x2, waiting for transfers between devices: 95.7 us -> 61 us  [gathered_by_axis(): nearer = lax.all_gather(x, axes[-1], axis=dim, tiled=True)]
    all_to_all x0 -> x1, starting transfers between devices: none -> 9.41 us  [per_device(): lax.all_to_all(jnp.stack([grad_out] * lax.axis_size('tensor')), 'tensor',...]
    another operation x0 -> x1, local copies, waits for them, and re-layouts: none -> 6.9 us  [per_device(): jnp.stack([grad_out] * lax.axis_size('tensor'))]
    reduce_scatter x2, waiting for transfers between devices: 68.3 us -> 73.7 us  [sum_by_axis(): subtotal = lax.psum_scatter(subtotal, axis, scatter_dimension=0, tiled=True)]
  transfers between devices with their start and end apart: 7 -> 7, of which waited for: 5 -> 4; matrix products, arithmetic and copies ran while one was open for 19% -> 17% of each run, Pallas kernels for 0% -> 0%
where the time goes in v1:
time: 451 us; the launch traced here: 450 us
  waiting for transfers between devices  342 us (76%)
  matrix products  69.8 us (15%)
  between operations  14 us (3%)
  starting transfers between devices  12.7 us (3%)
  local copies, waits for them, and re-layouts  11.1 us (2%)
    all_to_all x1, waiting for transfers between devices, per_device(): lax.all_to_all(jnp.stack([grad_out] * lax.axis_size('tensor')), 'tensor',...  201 us
    reduce_scatter x2, waiting for transfers between devices, sum_by_axis(): subtotal = lax.psum_scatter(subtotal, axis, scatter_dimension=0, tiled=True)  73.7 us
    all_gather x2, waiting for transfers between devices, gathered_by_axis(): nearer = lax.all_gather(x, axes[-1], axis=dim, tiled=True)  61 us
    dot_general x1, matrix products, per_device(): lax.dot_general(grad_block, attended, (((0,), (0,)), ((), ())), preferred...  17.5 us
    dot_general x1, matrix products, per_device(): jnp.dot(grad_block, gathered_by_axis(out_weight, DP, 0), preferred_elemen...  15.6 us
    dot_general x1, matrix products, attention_grads(): jnp.einsum('qgd,kd->gqk', grad_heads, value_one, preferred_element_type=j...  11.5 us
    all_to_all x1, starting transfers between devices, per_device(): lax.all_to_all(jnp.stack([grad_out] * lax.axis_size('tensor')), 'tensor',...  9.41 us
  transfers between devices with their start and end apart: 7, of which 4 were waited for; matrix products, arithmetic and copies ran while one was open for 17% of the time, Pallas kernels for 0%

profile of v1, /device:TPU:1, one launch (start us, length us, event | category | flops | bytes accessed | tf_op | source)
XLA Modules:
  0.0 450.3 jit_solution(6925256552827773162)
XLA Ops:
  7.2 0.0 copy-start
  7.2 6.9 %stack.8 = bf16[16,64,8192]{2,1,0:T(8,128)(2,1)} broadcast(bf16[64,8192]{1,0:T(8,128)(2,1)} %param.7), dimensions={1,2} | broadcast | bytes 17825792 | tf_op jit(solution)/shard_map/stack | solution.py:72
  14.1 0.0 copy-start.1
  14.1 9.4 %all-to-all-start = ((bf16[16,64,8192]{2,1,0:T(8,128)(2,1)}), bf16[16,64,8192]{2,1,0:T(8,128)(2,1)}, u32[]{:S(2)}, u32[]{:S(2)}) async-start(bf16[16,64,8192]{2,1,0:T(8,128)(2,1)} %stack.8), calls=%async_computation | async-start | bytes 33554432 | tf_op jit(solution)/shard_map/all_to_all | solution.py:72
  23.5 0.0 all-gather.3.cloned.1.call-start
  23.5 0.7 all-gather.3.cloned.1.call-update
  24.2 0.0 all-gather.5.cloned.1.call-start
  24.3 61.0 %all-gather.3.cloned.1.call-done = bf16[2048,512]{1,0:T(8,128)(2,1)} async-done(((bf16[1024,512]{1,0:T(8,128)(2,1)}), bf16[2048,512]{1,0:T(8,128)(2,1)}) %all-gather.3.cloned.1.call-update) | async-done | bytes 2097168 | tf_op jit(solution)/shard_map/all_gather | solution.py:17
  85.3 0.0 all-gather.5.cloned.1.call-update
  85.3 0.0 reduce-scatter.3.cloned.1.call-start
  85.4 200.8 %all-to-all-done = bf16[16,64,8192]{2,1,0:T(8,128)(2,1)} async-done(((bf16[16,64,8192]{2,1,0:T(8,128)(2,1)}), bf16[16,64,8192]{2,1,0:T(8,128)(2,1)}, u32[]{:S(2)}, u32[]{:S(2)}) %all-to-all-start) | async-done | bytes 16777248 | tf_op jit(solution)/shard_map/all_to_all | solution.py:72
  286.2 0.0 copy-done.1
  286.2 17.5 %convolution_convert_fusion = bf16[8192,512]{1,0:T(8,128)(2,1)} fusion(bf16[1024,8192]{1,0:T(8,128)(2,1)} %bitcast.4, bf16[1024,512]{1,0:T(8,128)(2,1)S(1)} %copy-done.1), kind=kOutput, calls=%fused_computation.7 | convolution fusion | flops 8594128896 | bytes 26214400 | tf_op jit(solution)/shard_map/dot_general | solution.py:80
  303.8 0.0 reduce-scatter.3.cloned.1.call-update
  303.8 0.2 reduce-scatter.5.cloned.1.call-start
  304.0 1.6 copy.26
  305.7 0.0 copy-done.2
  305.7 0.5 copy.27
  306.2 0.3 iota_compare_fusion
  306.5 0.0 copy-start.3
  306.5 0.0 copy-done
  306.6 8.1 %fusion.15 = f32[1024,1024,4]{1,0,2:T(8,128)} fusion(bf16[1024,4,128]{0,2,1:T(8,128)(2,1)S(1)} %bitcast.66, bf16[1024,512]{1,0:T(8,128)(2,1)S(1)} %copy-done, s32[]{:T(128)S(6)} %select_n.56), kind=kOutput, calls=%fused_computation.25 | convolution fusion | flops 1073741824 | bytes 18087940 | tf_op jit(solution)/shard_map/qgd,kd->gqk/dot_general | solution.py:43
  314.6 15.6 %multiply_reduce_fusion = (f32[1024,4]{0,1:T(4,128)S(1)}, bf16[1024,512]{0,1:T(8,128)(2,1)}) fusion(f32[1024,512]{0,1:T(8,128)} %copy.26, bf16[1024,8192]{1,0:T(8,128)(2,1)} %bitcast.4, bf16[8192,512]{1,0:T(8,128)(2,1)} %all-gather.5.cloned.1.call-done), kind=kOutput, calls=%fused_computation.12 | convolution fusion | flops 8592027648 | bytes 28327936 | tf_op jit(solution)/shard_map/dot_general | solution.py:75
  330.2 73.7 %reduce-scatter.3.cloned.1.call-done = bf16[2048,512]{1,0:T(8,128)(2,1)} async-done(((bf16[8192,512]{1,0:T(8,128)(2,1)}), bf16[2048,512]{1,0:T(8,128)(2,1)}) %reduce-scatter.3.cloned.1.call-update) | async-done | bytes 2097168 | tf_op jit(solution)/shard_map/reduce_scatter | solution.py:24
  403.9 0.0 reduce-scatter.5.cloned.1.call-update
  403.9 0.0 copy-done.3
  404.0 0.0 copy-done.4
  404.0 0.0 slice-start
  404.0 0.0 slice-start.1
  404.0 0.0 slice-start.2
  404.0 0.0 copy-start.5
  404.0 11.5 %fusion.1 = bf16[4,1024,1024]{1,2,0:T(8,128)(2,1)} fusion(f32[1024,1024,4]{1,0,2:T(8,128)} %fusion.15, bf16[1024,4,128]{0,2,1:T(8,128)(2,1)} %bitcast.68, f32[4,1024]{1,0:T(4,128)S(1)} %bitcast.70, f32[4,1024]{1,0:T(4,128)S(1)} %copy-done.4, pred[1024,1024]{0,1:T(8,128)(4,1)S(1)} %iota_compare_fusion, bf16[1024,512]{1,0:T(8,128)(2,1)} %param.11, ...), kind=kOutput, calls=%fused_computation.2 | convolution fusion | flops 1098907648 | bytes 27557892 | tf_op jit(solution)/shard_map/qgd,kd->gqk/dot_general | solution.py:48
  415.5 7.2 %fusion.9 = f32[1,1024,128]{1,2,0:T(8,128)S(1)} fusion(bf16[4,1024,1024]{1,2,0:T(8,128)(2,1)} %fusion.1, bf16[1024,4,128]{0,2,1:T(8,128)(2,1)S(1)} %bitcast.67), kind=kOutput, calls=%fused_computation.16 | convolution fusion | flops 1073872896 | bytes 9961472 | tf_op jit(solution)/shard_map/gqk,qgd->kd/dot_general | solution.py:61
  422.6 0.0 slice-done
  422.6 0.0 slice-done.1
  422.7 0.0 slice-done.2
  422.7 0.0 copy-done.5
  422.7 0.0 slice-done.3
  422.7 5.2 %fusion.10 = f32[1,1024,128]{1,2,0:T(8,128)S(1)} fusion(bf16[1024,4,128]{0,2,1:T(8,128)(2,1)S(1)} %bitcast.69, f32[1024,1024,4]{1,0,2:T(8,128)S(1)} %bitcast.64, f32[4,1024]{1,0:T(4,128)S(1)} %copy-done.4, pred[1024,1024]{0,1:T(8,128)(4,1)} %copy-done.3), kind=kOutput, calls=%fused_computation.17 | convolution fusion | flops 1090519040 | bytes 19415040 | tf_op jit(solution)/shard_map/gqk,qgd->kd/dot_general | solution.py:64
  427.9 0.1 select_convert_fusion
  428.0 1.5 collective-permute-start
  429.5 5.9 %collective-permute-done = bf16[2,1024,64]{1,2,0:T(8,128)(2,1)S(1)} collective-permute-done((bf16[2,1024,64]{1,2,0:T(8,128)(2,1)S(1)}, bf16[2,1024,64]{1,2,0:T(8,128)(2,1)S(1)}, u32[]{:S(2)}, u32[]{:S(2)}) %collective-permute-start) | collective-permute-done | bytes 262176 | tf_op jit(solution)/shard_map/ppermute | solution.py:31
  435.4 0.1 convert_add_fusion
  435.5 1.5 collective-permute-start.1
  437.0 4.7 %multiply_convert_fusion = bf16[128,4,1024]{2,0,1:T(8,128)(2,1)S(1)} fusion(bf16[4,1024,1024]{1,2,0:T(8,128)(2,1)} %fusion.1, bf16[1024,512]{1,0:T(8,128)(2,1)S(1)} %copy-done, s32[]{:T(128)S(6)} %select_n.56), kind=kOutput, calls=%fused_computation.11 | convolution fusion | flops 1074790400 | bytes 9699332 | tf_op jit(solution)/shard_map/gqk,kd->qgd/dot_general | solution.py:56
  441.7 1.3 copy.19
  443.1 0.0 collective-permute-done.1
  443.1 0.7 slice_bitcast_fusion
  (8 shorter events, 0.1 us)
Async XLA Ops:
  7.2 299.4 %copy-start = (bf16[1024,512]{1,0:T(8,128)(2,1)S(1)}, bf16[1024,512]{1,0:T(8,128)(2,1)}, u32[]{:S(2)}) copy-start(bf16[1024,512]{1,0:T(8,128)(2,1)} %param.10) | copy-start | bytes 3145732
  14.1 272.2 %copy-start.1 = (bf16[1024,512]{1,0:T(8,128)(2,1)S(1)}, bf16[1024,512]{1,0:T(8,128)(2,1)}, u32[]{:S(2)}) copy-start(bf16[1024,512]{1,0:T(8,128)(2,1)} %param.12) | copy-start | bytes 3145732
  14.1 272.2 %all-to-all-start = ((bf16[16,64,8192]{2,1,0:T(8,128)(2,1)}), bf16[16,64,8192]{2,1,0:T(8,128)(2,1)}, u32[]{:S(2)}, u32[]{:S(2)}) async-start(bf16[16,64,8192]{2,1,0:T(8,128)(2,1)} %stack.8), calls=%async_computation | async-start | bytes 33554432 | tf_op jit(solution)/shard_map/all_to_all | solution.py:72
  23.5 61.8 %all-gather.3.cloned.1.call-start = ((), (), s32[]{:S(2)}) async-start(), calls=%async_computation.3 | async-start | bytes 3145728 | tf_op jit(solution)/shard_map/all_gather | solution.py:17
  24.2 290.4 %all-gather.5.cloned.1.call-start = ((), (), s32[]{:S(2)}) async-start(), calls=%async_computation.4 | async-start | bytes 10485760 | tf_op jit(solution)/shard_map/all_gather | solution.py:17
  85.3 318.6 %reduce-scatter.3.cloned.1.call-start = ((), (), s32[]{:S(2)}) async-start(), calls=%async_computation.5 | async-start | bytes 10485760 | tf_op jit(solution)/shard_map/reduce_scatter | solution.py:24
  286.2 19.4 %copy-start.2 = (bf16[1024,512]{1,0:T(8,128)(2,1)S(1)}, bf16[1024,512]{1,0:T(8,128)(2,1)}, u32[]{:S(2)}) copy-start(bf16[1024,512]{1,0:T(8,128)(2,1)} %param.9) | copy-start | bytes 3145732
  303.8 139.9 %reduce-scatter.5.cloned.1.call-start = ((), (), s32[]{:S(2)}) async-start(), calls=%async_computation.6 | async-start | bytes 3145728 | tf_op jit(solution)/shard_map/reduce_scatter | solution.py:24
  306.5 97.4 %copy-start.3 = (pred[1024,1024]{0,1:T(8,128)(4,1)}, pred[1024,1024]{0,1:T(8,128)(4,1)S(1)}, u32[]{:S(2)}) copy-start(pred[1024,1024]{0,1:T(8,128)(4,1)S(1)} %iota_compare_fusion) | copy-start | bytes 3145732
  314.6 89.3 %copy-start.4 = (f32[4,1024]{1,0:T(4,128)S(1)}, f32[4,1024]{1,0:T(4,128)}, u32[]{:S(2)}) copy-start(f32[4,1024]{1,0:T(4,128)} %param.13) | copy-start | bytes 49156
  404.0 18.7 %slice-start = ((s8[16777216]{0:T(1024)(128)(4,1)}), s8[4194304]{0:T(1024)(128)(4,1)S(1)}, s32[]{:S(2)}) async-start(s8[16777216]{0:T(1024)(128)(4,1)} %bitcast.63), calls=%async_computation.7 | async-start | bytes 8388608
  404.0 18.7 %slice-start.1 = ((s8[16777216]{0:T(1024)(128)(4,1)}), s8[4194304]{0:T(1024)(128)(4,1)S(1)}, s32[]{:S(2)}) async-start(s8[16777216]{0:T(1024)(128)(4,1)} %bitcast.63), calls=%async_computation.8 | async-start | bytes 8388608
  404.0 18.7 %slice-start.2 = ((s8[16777216]{0:T(1024)(128)(4,1)}), s8[4194304]{0:T(1024)(128)(4,1)S(1)}, s32[]{:S(2)}) async-start(s8[16777216]{0:T(1024)(128)(4,1)} %bitcast.63), calls=%async_computation.9 | async-start | bytes 8388608
  404.0 18.7 %copy-start.5 = (bf16[1024,512]{0,1:T(8,128)(2,1)S(1)}, bf16[1024,512]{0,1:T(8,128)(2,1)}, u32[]{:S(2)}) copy-start(bf16[1024,512]{0,1:T(8,128)(2,1)} %get-tuple-element.11) | copy-start | bytes 3145732
  415.5 7.2 %slice-start.3 = ((s8[16777216]{0:T(1024)(128)(4,1)}), s8[4194304]{0:T(1024)(128)(4,1)S(1)}, s32[]{:S(2)}) async-start(s8[16777216]{0:T(1024)(128)(4,1)} %bitcast.63), calls=%async_computation.10 | async-start | bytes 8388608
  428.0 7.4 %collective-permute-start = (bf16[2,1024,64]{1,2,0:T(8,128)(2,1)S(1)}, bf16[2,1024,64]{1,2,0:T(8,128)(2,1)S(1)}, u32[]{:S(2)}, u32[]{:S(2)}) collective-permute-start(bf16[2,1024,64]{1,2,0:T(8,128)(2,1)S(1)} %select_convert_fusion), channel_id=1, source_target_pairs={{0,2},{1,3},{2,0},{3,1},{4,6},{5,7},{6,4},{7,5},{8,10},{9,11},{10,... | collective-permute-start | bytes 786440 | tf_op jit(solution)/shard_map/ppermute | solution.py:31
  435.5 7.5 %collective-permute-start.1 = (bf16[2,1024,32]{1,2,0:T(8,128)(2,1)S(1)}, bf16[2,1024,32]{1,2,0:T(8,128)(2,1)S(1)}, u32[]{:S(2)}, u32[]{:S(2)}) collective-permute-start(bf16[2,1024,32]{1,2,0:T(8,128)(2,1)S(1)} %select_convert_fusion.1), channel_id=1, source_target_pairs={{0,1},{1,0},{2,3},{3,2},{4,5},{5,4},{6,7},{7,6},{8,9},{9,8},{10,11... | collective-permute-start | bytes 393224 | tf_op jit(solution)/shard_map/ppermute | solution.py:31
Sparse Core Ops, SparseCore 0:
  26.0 59.3 all-gather.2
  87.0 83.8 all-gather.4
  303.9 99.9 reduce-scatter.2
  406.7 34.0 reduce-scatter.4
